TPU v7x, 512 devices: a whole 4x8x8 slice. The times are simulated.
512 devices in a mesh: clus: 16 (over x_lo, z), seq: 32 (over y, x_hi, core).
Axes of the slice: x: 4 (x_hi: 2, x_lo: 2; x = x_hi * 2 + x_lo), y: 8, z: 8, core: 2. Of those that a mesh axis runs over, the one named last changes fastest.
Arguments:
- embeddings: bfloat16 [131072, 768], P(('clus', 'seq')), parts along dimension 0, may hold values from -1 to 1, as said below
- doc_order: int32 [512, 256], P(('clus', 'seq')), parts along dimension 0, may hold values from 0 to 255, each once within a row
Outputs:
- prior_max: float32 [131072], P(('clus', 'seq')), parts along dimension 0
- later_max: float32 [131072], P(('clus', 'seq')), parts along dimension 0
There are 16 independent parts, one for each index of `clus`. A program takes and returns all parts, laid end to end along the dimension named above; each array names one. Nothing has to cross between parts.
Inputs may be any that keep to these rules, and one draw needn't show every extreme that they name: `embeddings`: each row has unit Euclidean length up to bfloat16 rounding. `doc_order`: each row is a permutation of 0 to 255.
All inputs are finite; a program needn't handle non-finite values.
Results may differ from a plain program's by a relative error of at most 0.0003.
Values may be sent and summed in bfloat16 or wider, within the bound.
A program may use at most 64 MiB of HBM per device.

v0:
```python
import jax
import jax.numpy as jnp
from jax import lax
from jax.sharding import PartitionSpec as P


def similar(left_rows, right_rows):
    return jnp.einsum("rd,cd->rc", left_rows, right_rows, preferred_element_type=jnp.float32)


def masked_rowmax(matrix, keep):
    return jnp.max(jnp.where(keep, matrix, jnp.float32(-1.0)), axis=1)


def per_device(embeddings, doc_order):
    ranking = doc_order[0]
    position = lax.axis_index("seq")
    block_rows = embeddings.shape[0]
    self_sims = similar(embeddings, embeddings)
    prior_start = masked_rowmax(self_sims, ranking[None, :] < ranking[:, None])
    later_start = masked_rowmax(self_sims, ranking[None, :] > ranking[:, None])
    incoming = lax.all_gather(embeddings, "seq", axis=0, tiled=True)
    block_of = jnp.arange(incoming.shape[0], dtype=jnp.int32) // block_rows
    sims_here = similar(embeddings, incoming)
    before = (block_of < position)[None, :]
    after = (block_of > position)[None, :]
    prior_max = jnp.maximum(prior_start, masked_rowmax(sims_here, before))
    later_max = jnp.maximum(later_start, masked_rowmax(sims_here, after))
    return (prior_max, later_max)


def solution(mesh):
    return jax.shard_map(
        per_device,
        mesh=mesh,
        in_specs=(P(("clus", "seq"), None), P(("clus", "seq"), None)),
        out_specs=(P(("clus", "seq")), P(("clus", "seq"))),
        check_vma=False,
    )
```

profile of v0, /device:TPU:1, one launch (start us, length us, event | category | flops | bytes accessed | tf_op | source)
XLA Modules:
  0.0 155.9 jit_solution(16128847913500054995)
XLA Ops:
  7.2 0.0 all-gather.2.cloned.1.call-start
  7.2 0.7 all-gather.2.cloned.1.call-update
  7.9 1.5 select_reduce_fusion.2
  9.4 130.2 %all-gather.2.cloned.1.call-done = bf16[8192,768]{1,0:T(8,128)(2,1)} async-done(((bf16[256,768]{1,0:T(8,128)(2,1)}), bf16[8192,768]{1,0:T(8,128)(2,1)}) %all-gather.2.cloned.1.call-update) | async-done | bytes 12582928 | tf_op jit(solution)/shard_map/all_gather | solution.py:22
  139.6 8.3 %select_reduce_fusion = (f32[256]{0:T(256)S(1)}, f32[256]{0:T(256)S(1)}) fusion(pred[8192]{0:T(1024)(128)(4,1)S(1)} %get-tuple-element.6, pred[8192]{0:T(1024)(128)(4,1)S(1)} %get-tuple-element.7, bf16[256,768]{1,0:T(8,128)(2,1)} %param.2, bf16[8192,768]{1,0:T(8,128)(2,1)} %all-gather.2.cloned.1.call-done), kind=kOutput, calls=%fused_computation | convolution fusion | flops 3229613568 | bytes 12994560 | tf_op jit(solution)/shard_map/rd,cd->rc/dot_general | solution.py:8
  147.9 0.6 max.7
  148.5 0.6 max.6
  (1 shorter events, 0.0 us)
Async XLA Ops:
  7.2 132.4 %all-gather.2.cloned.1.call-start = ((), (), s32[]{:S(2)}) async-start(), calls=%async_computation | async-start | bytes 12976128 | tf_op jit(solution)/shard_map/all_gather | solution.py:22
Sparse Core Ops, SparseCore 0:
  11.3 128.2 all-gather.1
where the time goes:
time: 156 us
  waiting for transfers between devices  131 us (84%)
  between operations  14 us (9%)
  matrix products  9.76 us (6%)
    all_gather x1, waiting for transfers between devices, per_device(): incoming = lax.all_gather(embeddings, 'seq', axis=0, tiled=True)  130 us
    dot_general x2, matrix products, similar(): jnp.einsum('rd,cd->rc', left_rows, right_rows, preferred_element_type=jnp...  9.76 us
  transfers between devices with their start and end apart: 1, of which 1 were waited for; matrix products, arithmetic and copies ran while one was open for 1% of the time, Pallas kernels for 0%

commit v1 on v0

v1 whole, which is shorter than its diff:
```python
import jax
import jax.numpy as jnp
from jax import lax
from jax.experimental import pallas as pl
from jax.experimental.pallas import tpu as pltpu
from jax.sharding import PartitionSpec as P

MESH = pl.DeviceIdType.MESH
CHUNKS = 4
YS = 8


def sims(left, right):
    return lax.dot_general(left, right, (((1,), (1,)), ((), ())), preferred_element_type=jnp.float32)


def colmax(s):
    return jnp.max(s, axis=0, keepdims=True)


def lanes(s):
    out = s[:, :128]
    for j in range(1, s.shape[1] // 128):
        out = jnp.maximum(out, s[:, j * 128 : (j + 1) * 128])
    return out


def flip(r):
    return jnp.max(jnp.transpose(r), axis=0, keepdims=True)


def kernel(emb, order, out, own, m1, m2, pc, e, own2, rank, msg_out, msg_in,
           csem, s_ring, r_ring, s_sib, r_sib, s_msg, r_msg):
    clus = lax.axis_index("clus")
    seq = lax.axis_index("seq")
    y, h, c = seq // 4, (seq // 2) % 2, seq % 2

    def dev(dy, hh, cc):
        return (clus, ((y + dy + YS) % YS) * 4 + hh * 2 + cc)

    up, down = dev(1, h, c), dev(-1, h, c)
    across, sib = dev(0, 1 - h, c), dev(0, h, 1 - c)
    rows = own.shape[0] // CHUNKS

    def part(k):
        return pl.ds(k * rows, rows)

    load = pltpu.make_async_copy(emb, own, csem.at[0])
    load_rank = pltpu.make_async_copy(order, rank, csem.at[1])
    load.start()
    load_rank.start()
    barrier = pltpu.get_barrier_semaphore()
    for d in (up, down, across, sib):
        pl.semaphore_signal(barrier, inc=1, device_id=d, device_id_type=MESH)
    pl.semaphore_wait(barrier, 4)
    load.wait()
    load_rank.wait()

    sent = []

    def send(src, dst, s, r, d):
        copy = pltpu.make_async_remote_copy(
            src_ref=src, dst_ref=dst, send_sem=s, recv_sem=r, device_id=d, device_id_type=MESH
        )
        sent.append(copy)
        return copy

    ring = lambda i, k: (s_ring.at[i, k], r_ring.at[i, k])
    near = lambda i, k: (s_sib.at[i, k], r_sib.at[i, k])
    c_m1 = [send(own.at[part(k)], m1.at[part(k)], *ring(0, k), up) for k in range(CHUNKS)]
    c_p1 = [send(own.at[part(k)], pc.at[0, c, part(k)], *ring(1, k), down) for k in range(CHUNKS)]
    c_m2 = [send(m1.at[part(k)], m2.at[part(k)], *ring(2, k), up) for k in range(CHUNKS)]
    which = ((y + 7) % YS) // 4
    c_e = [send(pc.at[which, c, part(k)], e.at[c, part(k)], *ring(3, k), down) for k in range(CHUNKS)]
    c_c1 = [send(pc.at[0, c, part(k)], pc.at[1, c, part(k)], *ring(4, k), across) for k in range(CHUNKS)]
    c_own = send(own, own2, *near(0, 0), sib)
    n_p1 = [send(pc.at[0, c, part(k)], pc.at[0, c, part(k)], *near(1, k), sib) for k in range(CHUNKS)]
    n_c1 = [send(pc.at[1, c, part(k)], pc.at[1, c, part(k)], *near(2, k), sib) for k in range(CHUNKS)]
    n_e = [send(e.at[c, part(k)], e.at[c, part(k)], *near(3, k), sib) for k in range(CHUNKS)]

    for k in range(CHUNKS):
        c_m1[k].start()
        c_p1[k].start()
    c_own.start()

    neg = jnp.float32(-1.0)
    rank_cols = jnp.broadcast_to(rank[...].astype(jnp.float32), (256, 256))
    rank_rows = jnp.transpose(rank_cols)
    s = sims(own[...], own[...])
    prior0 = colmax(jnp.where(rank_rows < rank_cols, s, neg))
    later0 = colmax(jnp.where(rank_rows > rank_cols, s, neg))

    for k in range(CHUNKS):
        c_m1[k].wait_recv()
        c_m2[k].start()
        c_p1[k].wait_recv()
        c_c1[k].start()
        n_p1[k].start()
        if k >= 1:
            c_c1[k - 1].wait_recv()
            c_e[k - 1].start()
            n_c1[k - 1].start()
    k = CHUNKS - 1
    c_c1[k].wait_recv()
    c_e[k].start()
    n_c1[k].start()

    c_own.wait_recv()
    s01 = colmax(sims(own2[...], own[...]))
    prior0 = jnp.maximum(prior0, jnp.where(c == 1, s01, neg))
    later0 = jnp.maximum(later0, jnp.where(c == 0, s01, neg))

    for k in range(CHUNKS):
        n_p1[k].wait_recv()

    def meet(a, kind, col):
        r = None
        for j in range(2):
            s = sims(a, pc[kind, j])
            col.append(colmax(s))
            r = lanes(s) if r is None else jnp.maximum(r, lanes(s))
        return r

    col0, col1, col2 = [], [], []
    r0 = meet(own[...], 0, col0)
    r1 = meet(m1[...], 0, col1)
    for k in range(CHUNKS):
        n_c1[k].wait_recv()
    r0 = jnp.maximum(r0, meet(own[...], 1, col0))
    r1 = jnp.maximum(r1, meet(m1[...], 1, col1))
    other = (c + h) % 2
    pblk, cblk = pc[0, c], pc[1, other]
    pcol = colmax(sims(cblk, pblk))
    ccol = colmax(sims(pblk, cblk))
    r0, r1 = flip(r0), flip(r1)

    for k in range(CHUNKS):
        c_e[k].wait_recv()
        n_e[k].start()
    for k in range(CHUNKS):
        c_m2[k].wait_recv()
    r2 = meet(m2[...], 0, col2)
    r2 = flip(jnp.maximum(r2, meet(m2[...], 1, col2)))
    ecol, re = [], None
    for k in range(CHUNKS):
        n_e[k].wait_recv()
    for j in range(2):
        s = sims(m2[...], e[j])
        ecol.append(colmax(s))
        re = lanes(s) if re is None else jnp.maximum(re, lanes(s))
    re = flip(re)

    at = lambda dy: (y + dy + YS) % YS
    first0, first1, first2, first2e = at(0) < at(1), at(-1) < at(1), at(-2) < at(1), at(-2) < at(2)

    def pick(flag, v):
        return jnp.where(flag, v, neg)

    def top(*vs):
        o = vs[0]
        for v in vs[1:]:
            o = jnp.maximum(o, v)
        return o

    prior0 = top(prior0, pick(~first0, r0))
    later0 = top(later0, pick(first0, r0))

    def put(i, prior, later):
        msg_out[i, 0:1, :] = jnp.maximum(prior, neg)
        msg_out[i, 1:2, :] = jnp.maximum(later, neg)

    put(0, pick(~first1, r1), pick(first1, r1))
    put(1, top(pick(~first2, r2), pick(~first2e, re)), top(pick(first2, r2), pick(first2e, re)))
    for j in range(2):
        x = [col0[j], col1[j], col2[j]]
        mine = pick(c == j, pcol)
        put(2 + j,
            top(pick(h == 1, mine), *[pick(f, v) for f, v in zip((first0, first1, first2), x)]),
            top(pick(h == 0, mine), *[pick(~f, v) for f, v in zip((first0, first1, first2), x)]))
        x = [col0[2 + j], col1[2 + j], col2[2 + j]]
        mine = pick(other == j, ccol)
        put(4 + j,
            top(pick(h == 0, mine), *[pick(f, v) for f, v in zip((first0, first1, first2), x)]),
            top(pick(h == 1, mine), *[pick(~f, v) for f, v in zip((first0, first1, first2), x)]))
        put(6 + j, pick(first2e, ecol[j]), pick(~first2e, ecol[j]))

    he = (h + y // 4) % 2
    results = []
    for i, slot, d in [
        (0, 0, dev(-1, h, c)), (1, 1, dev(-2, h, c)),
        (2, 2 + c, dev(1, h, 0)), (3, 2 + c, dev(1, h, 1)),
        (4, 4 + c, dev(1, 1 - h, 0)), (5, 4 + c, dev(1, 1 - h, 1)),
        (6, 6 + c, dev(2, he, 0)), (7, 6 + c, dev(2, he, 1)),
    ]:
        copy = send(msg_out.at[i], msg_in.at[slot], s_msg.at[i], r_msg.at[slot], d)
        copy.start()
        results.append(copy)
    for i in range(8):
        pltpu.make_async_remote_copy(
            src_ref=msg_out.at[i], dst_ref=msg_in.at[i], send_sem=s_msg.at[i], recv_sem=r_msg.at[i],
            device_id=up, device_id_type=MESH,
        ).wait_recv()
    got = msg_in[...]
    best = jnp.max(got, axis=0)
    out[...] = jnp.maximum(best, jnp.concatenate([prior0, later0], axis=0))
    for copy in sent:
        copy.wait_send()


def per_device(embeddings, doc_order):
    rows, width = embeddings.shape
    block = (rows, width)
    vm = lambda *lead: pltpu.VMEM((*lead, *block), jnp.bfloat16)
    dma = lambda *n: pltpu.SemaphoreType.DMA(n)
    both = pl.pallas_call(
        kernel,
        name="dedup",
        out_shape=jax.ShapeDtypeStruct((2, rows), jnp.float32),
        in_specs=[pl.BlockSpec(memory_space=pl.ANY)] * 2,
        out_specs=pl.BlockSpec(memory_space=pltpu.VMEM),
        scratch_shapes=[
            vm(), vm(), vm(), vm(2, 2), vm(2), vm(),
            pltpu.VMEM((1, rows), jnp.int32),
            pltpu.VMEM((8, 2, rows), jnp.float32),
            pltpu.VMEM((8, 2, rows), jnp.float32),
            dma(2), dma(5, CHUNKS), dma(5, CHUNKS), dma(4, CHUNKS), dma(4, CHUNKS), dma(8), dma(8),
        ],
        compiler_params=pltpu.CompilerParams(
            collective_id=0, has_side_effects=True, vmem_limit_bytes=32 * 1024 * 1024
        ),
    )(embeddings, doc_order)
    return both[0], both[1]


def solution(mesh):
    return jax.shard_map(
        per_device,
        mesh=mesh,
        in_specs=(P(("clus", "seq"), None), P(("clus", "seq"), None)),
        out_specs=(P(("clus", "seq")), P(("clus", "seq"))),
        check_vma=False,
    )
```

time: 156 us -> 38.7 us (0.25)
  waiting for transfers between devices: 131 us -> 0 us
  Pallas kernels: 0 us -> 35.7 us
  between operations: 14 us -> 0.65 us
  matrix products: 9.76 us -> 0 us
  local copies, waits for them, and re-layouts: 0 us -> 2.24 us
    all_gather x1 -> x0, waiting for transfers between devices: 130 us -> none  [per_device(): incoming = lax.all_gather(embeddings, 'seq', axis=0, tiled=True)]
    pallas_call x0 -> x1, Pallas kernels: none -> 35.7 us  [per_device(): pl.pallas_call(kernel, name='dedup', out_shape=jax.ShapeDtypeStruct((2, r...]
    dot_general x2 -> x0, matrix products: 9.76 us -> none  [similar(): jnp.einsum('rd,cd->rc', left_rows, right_rows, preferred_element_type=jnp...]
    unnamed x0 -> x4, local copies, waits for them, and re-layouts: none -> 1.67 us
  transfers between devices with their start and end apart: 1 -> 0, of which waited for: 1 -> 0; matrix products, arithmetic and copies ran while one was open for 1% -> 0% of each run, Pallas kernels for 0% -> 0%
where the time goes in v1:
time: 38.7 us; the launch traced here: 38.5 us
  Pallas kernels  35.7 us (92%)
  local copies, waits for them, and re-layouts  2.24 us (6%)
  between operations  0.65 us (2%)
    pallas_call x1, Pallas kernels, per_device(): pl.pallas_call(kernel, name='dedup', out_shape=jax.ShapeDtypeStruct((2, r...  35.7 us
    unnamed x4, local copies, waits for them, and re-layouts  1.67 us

profile of v1, /device:TPU:1, one launch (start us, length us, event | category | flops | bytes accessed | tf_op | source)
XLA Modules:
  0.0 38.5 jit_solution(14951656842299491741)
XLA Ops:
  0.6 0.0 copy-start
  0.6 1.0 %copy-done = bf16[256,768]{1,0:T(8,128)(2,1)S(1)} copy-done((bf16[256,768]{1,0:T(8,128)(2,1)S(1)}, bf16[256,768]{1,0:T(8,128)(2,1)}, u32[]{:S(2)}) %copy-start) | copy-done | bytes 393240
  1.6 0.0 copy-start.1
  1.6 0.7 %copy-done.1 = s32[1,256]{1,0:T(1,128)S(1)} copy-done((s32[1,256]{1,0:T(1,128)S(1)}, s32[1,256]{1,0:T(1,128)}, u32[]{:S(2)}) %copy-start.1) | copy-done | bytes 1048
  2.3 35.7 %dedup.1 = f32[2,256]{1,0:T(2,128)S(1)} custom-call(bf16[256,768]{1,0:T(8,128)(2,1)S(1)} %copy-done, s32[1,256]{1,0:T(1,128)S(1)} %copy-done.1), custom_call_target="tpu_custom_call" | custom-call | tf_op jit(solution)/shard_map/dedup/pallas_call | solution.py:215
  38.0 0.6 %fusion = (f32[1,256]{1,0:T(1,128)}, f32[1,256]{1,0:T(1,128)}) fusion(f32[2,256]{1,0:T(2,128)S(1)} %dedup.1), kind=kLoop, calls=%fused_computation | loop fusion | bytes 4096 | tf_op jit(solution)/shard_map/slice | solution.py:232
Async XLA Ops:
  0.6 1.0 %copy-start = (bf16[256,768]{1,0:T(8,128)(2,1)S(1)}, bf16[256,768]{1,0:T(8,128)(2,1)}, u32[]{:S(2)}) copy-start(bf16[256,768]{1,0:T(8,128)(2,1)} %emb.1) | copy-start | bytes 1179652
  1.6 0.7 %copy-start.1 = (s32[1,256]{1,0:T(1,128)S(1)}, s32[1,256]{1,0:T(1,128)}, u32[]{:S(2)}) copy-start(s32[1,256]{1,0:T(1,128)} %order.1) | copy-start | bytes 3076

commit v2 on v1

v2 whole, which is shorter than its diff:
```python
import jax
import jax.numpy as jnp
from jax import lax
from jax.experimental import pallas as pl
from jax.experimental.pallas import tpu as pltpu
from jax.sharding import PartitionSpec as P

MESH = pl.DeviceIdType.MESH
CHUNKS = 8
LAG = CHUNKS // 2
OPEN = 2
DELTA = 3
YS = 8


def sims(left, right):
    return lax.dot_general(left, right, (((1,), (1,)), ((), ())), preferred_element_type=jnp.float32)


def colmax(s):
    return jnp.max(s, axis=0, keepdims=True)


def lanes(s):
    out = s[:, :128]
    for j in range(1, s.shape[1] // 128):
        out = jnp.maximum(out, s[:, j * 128 : (j + 1) * 128])
    return out


def flip(r):
    return jnp.max(jnp.transpose(r), axis=0, keepdims=True)


def kernel(emb, order, out, own, m1, m2, pc, e, own2, rank, msg_out,
           hello, csem, s_sem, r_ring, r_all):
    clus = lax.axis_index("clus")
    seq = lax.axis_index("seq")
    y, h, c = seq // 4, (seq // 2) % 2, seq % 2

    def dev(dy, hh, cc):
        return (clus, ((y + dy + YS) % YS) * 4 + hh * 2 + cc)

    up, down = dev(1, h, c), dev(-1, h, c)
    across, sib = dev(0, 1 - h, c), dev(0, h, 1 - c)
    rows = own.shape[0] // CHUNKS

    def part(k):
        return pl.ds(k * rows, rows)

    even = (y + h + c) % 2 == 0
    odd = jnp.logical_not(even)
    no = jnp.logical_not
    corner = (clus == 0) & (c == 0)
    late_m1 = corner & (h == 0) & (y == 1)
    late_p1 = corner & (h == 0) & (y == YS - 1)
    late_c1 = corner & (h == 1) & ((y == 0) | (y == YS - 1))

    def signal(sem, *devices):
        for d in devices:
            pl.semaphore_signal(sem, inc=1, device_id=d, device_id_type=MESH)

    barrier = pltpu.get_barrier_semaphore()
    load = pltpu.make_async_copy(emb, own, csem.at[0])
    load_rank = pltpu.make_async_copy(order, rank, csem.at[1])
    load.start()
    load_rank.start()
    pl.when(even)(lambda: signal(barrier, across, sib))
    pl.when(odd)(lambda: signal(barrier, up, down))

    @pl.when(even)
    def _():
        pl.semaphore_wait(barrier, 2)
        signal(hello.at[0], down)
        signal(hello.at[1], up)

    load.wait()

    def copy(src, dst, stream, r, d):
        return pltpu.make_async_remote_copy(
            src_ref=src, dst_ref=dst, send_sem=s_sem.at[stream], recv_sem=r, device_id=d, device_id_type=MESH
        )

    which = ((y + 1) % YS) // 4
    every = range(CHUNKS)
    c_m1 = [copy(own.at[part(k)], m1.at[part(k)], 0, r_ring.at[0, k], up) for k in every]
    c_p1 = [copy(own.at[part(k)], pc.at[0, c, part(k)], 1, r_ring.at[1, k], down) for k in every]
    c_m2 = [copy(m1.at[part(k)], m2.at[part(k)], 2, r_all.at[0], up) for k in every]
    c_e = [copy(pc.at[which, c, part(k)], e.at[c, part(k)], 3, r_ring.at[3, k], down) for k in every]
    c_c1 = [copy(pc.at[0, c, part(k)], pc.at[1, c, part(k)], 4, r_ring.at[2, k], across) for k in every]
    c_own = copy(own, own2, 5, r_all.at[1], sib)
    n_p1 = [copy(pc.at[0, c, part(k)], pc.at[0, c, part(k)], 6, r_all.at[2], sib) for k in every]
    n_c1 = [copy(pc.at[1, c, part(k)], pc.at[1, c, part(k)], 7, r_all.at[3], sib) for k in every]
    n_e = [copy(e.at[c, part(k)], e.at[c, part(k)], 8, r_all.at[4], sib) for k in every]

    def take_all(i, dst):
        copy(own, dst, 0, r_all.at[i], up).wait_recv()

    def when(flag, *copies):
        @pl.when(flag)
        def _():
            for one in copies:
                one.start()

    when(even, *[one for pair in zip(c_m1, c_p1) for one in pair])

    def open_up():
        pl.semaphore_wait(hello.at[0], 1)
        for one in c_m1:
            one.start()

    def open_down():
        pl.semaphore_wait(hello.at[1], 1)
        for one in c_p1:
            one.start()

    @pl.when(odd & (y < YS // 2))
    def _():
        open_up()
        open_down()

    @pl.when(odd & (y >= YS // 2))
    def _():
        open_down()
        open_up()

    load_rank.wait()

    neg = jnp.float32(-1.0)
    rank_cols = jnp.broadcast_to(rank[...].astype(jnp.float32), (256, 256))
    rank_rows = jnp.transpose(rank_cols)
    s = sims(own[...], own[...])
    prior0 = colmax(jnp.where(rank_rows < rank_cols, s, neg))
    later0 = colmax(jnp.where(rank_rows > rank_cols, s, neg))

    @pl.when(odd)
    def _():
        pl.semaphore_wait(barrier, 2)
        signal(hello.at[2], across)
        signal(hello.at[3], sib)

    pl.when(even)(lambda: pl.semaphore_wait(hello.at[3], 1))
    c_own.start()

    def take_m1(k):
        c_m1[k].wait_recv()
        c_m2[k].start()

    def take_p1(k):
        c_p1[k].wait_recv()
        if k < OPEN:
            when(odd, c_c1[k])
        else:
            c_c1[k].start()
        when(which == 0, c_e[k])
        n_p1[k].start()

    def take_c1(k):
        c_c1[k].wait_recv()
        when(which == 1, c_e[k])
        n_c1[k].start()

    def turn(late, take, k):
        if 0 <= k < CHUNKS:
            pl.when(no(late))(lambda: take(k))
        if 0 <= k - DELTA < CHUNKS:
            pl.when(late)(lambda: take(k - DELTA))

    for k in range(CHUNKS + LAG + DELTA):
        if k == OPEN:
            pl.when(even)(lambda: pl.semaphore_wait(hello.at[2], 1))
            when(even, *c_c1[:OPEN])
        turn(late_m1, take_m1, k)
        turn(late_p1, take_p1, k)
        turn(late_c1, take_c1, k - LAG)

    c_own.wait_recv()
    s01 = colmax(sims(own2[...], own[...]))
    prior0 = jnp.maximum(prior0, jnp.where(c == 1, s01, neg))
    later0 = jnp.maximum(later0, jnp.where(c == 0, s01, neg))

    take_all(2, pc.at[0, 1 - c])

    def meet(a, kind, col):
        r = None
        for j in range(2):
            s = sims(a, pc[kind, j])
            col.append(colmax(s))
            r = lanes(s) if r is None else jnp.maximum(r, lanes(s))
        return r

    col0, col1, col2 = [], [], []
    r0 = meet(own[...], 0, col0)
    r1 = meet(m1[...], 0, col1)
    take_all(3, pc.at[1, 1 - c])
    r0 = jnp.maximum(r0, meet(own[...], 1, col0))
    r1 = jnp.maximum(r1, meet(m1[...], 1, col1))
    other = (c + h) % 2
    pblk, cblk = pc[0, c], pc[1, other]
    pcol = colmax(sims(cblk, pblk))
    ccol = colmax(sims(pblk, cblk))
    r0, r1 = flip(r0), flip(r1)

    for k in range(CHUNKS):
        c_e[k].wait_recv()
        n_e[k].start()
    take_all(0, m2)
    r2 = meet(m2[...], 0, col2)
    r2 = flip(jnp.maximum(r2, meet(m2[...], 1, col2)))
    ecol, re = [], None
    take_all(4, e.at[1 - c])
    for j in range(2):
        s = sims(m2[...], e[j])
        ecol.append(colmax(s))
        re = lanes(s) if re is None else jnp.maximum(re, lanes(s))
    re = flip(re)

    at = lambda dy: (y + dy + YS) % YS
    first0, first1, first2, first2e = at(0) < at(1), at(-1) < at(1), at(-2) < at(1), at(-2) < at(2)

    def pick(flag, v):
        return jnp.where(flag, v, neg)

    def top(*vs):
        o = vs[0]
        for v in vs[1:]:
            o = jnp.maximum(o, v)
        return o

    prior0 = top(prior0, pick(~first0, r0))
    later0 = top(later0, pick(first0, r0))

    def put(i, prior, later):
        msg_out[i, 0:1, :] = jnp.maximum(prior, neg)
        msg_out[i, 1:2, :] = jnp.maximum(later, neg)

    put(0, pick(~first1, r1), pick(first1, r1))
    put(1, top(pick(~first2, r2), pick(~first2e, re)), top(pick(first2, r2), pick(first2e, re)))
    for j in range(2):
        x = [col0[j], col1[j], col2[j]]
        mine = pick(c == j, pcol)
        put(2 + j,
            top(pick(h == 1, mine), *[pick(f, v) for f, v in zip((first0, first1, first2), x)]),
            top(pick(h == 0, mine), *[pick(~f, v) for f, v in zip((first0, first1, first2), x)]))
        x = [col0[2 + j], col1[2 + j], col2[2 + j]]
        mine = pick(other == j, ccol)
        put(4 + j,
            top(pick(h == 0, mine), *[pick(f, v) for f, v in zip((first0, first1, first2), x)]),
            top(pick(h == 1, mine), *[pick(~f, v) for f, v in zip((first0, first1, first2), x)]))
        put(6 + j, pick(first2e, ecol[j]), pick(~first2e, ecol[j]))

    put(8, prior0, later0)
    mine_out = pltpu.make_async_copy(msg_out.at[8], out.at[8], csem.at[0])
    mine_out.start()
    he = (h + ((y + 2) % YS) // 4) % 2
    for i, slot, d in [
        (0, 0, dev(-1, h, c)), (1, 1, dev(-2, h, c)),
        (2, 2 + c, dev(1, h, 0)), (3, 2 + c, dev(1, h, 1)),
        (4, 4 + c, dev(1, 1 - h, 0)), (5, 4 + c, dev(1, 1 - h, 1)),
        (6, 6 + c, dev(2, he, 0)), (7, 6 + c, dev(2, he, 1)),
    ]:
        copy(msg_out.at[i], out.at[slot], 9, r_all.at[5], d).start()
    copy(msg_out.at[0:8], out.at[0:8], 9, r_all.at[5], up).wait_recv()
    for stream in range(9):
        copy(own, m1, stream, r_all.at[0], up).wait_send()
    copy(msg_out.at[0:8], out.at[0:8], 9, r_all.at[5], up).wait_send()
    mine_out.wait()


def per_device(embeddings, doc_order):
    rows, width = embeddings.shape
    block = (rows, width)
    vm = lambda *lead: pltpu.VMEM((*lead, *block), jnp.bfloat16)
    dma = lambda *n: pltpu.SemaphoreType.DMA(n)
    both = pl.pallas_call(
        kernel,
        name="dedup",
        out_shape=jax.ShapeDtypeStruct((9, 2, rows), jnp.float32),
        in_specs=[pl.BlockSpec(memory_space=pltpu.HBM)] * 2,
        out_specs=pl.BlockSpec(memory_space=pl.ANY),
        scratch_shapes=[
            vm(), vm(), vm(), vm(2, 2), vm(2), vm(),
            pltpu.VMEM((1, rows), jnp.int32),
            pltpu.VMEM((9, 2, rows), jnp.float32),
            pltpu.SemaphoreType.REGULAR((4,)), dma(2), dma(10), dma(4, CHUNKS), dma(6),
        ],
        compiler_params=pltpu.CompilerParams(
            collective_id=0, has_side_effects=True
        ),
    )(embeddings, doc_order)
    return jnp.max(both[:, 0], axis=0), jnp.max(both[:, 1], axis=0)


def solution(mesh):
    return jax.shard_map(
        per_device,
        mesh=mesh,
        in_specs=(P(("clus", "seq"), None), P(("clus", "seq"), None)),
        out_specs=(P(("clus", "seq")), P(("clus", "seq"))),
        check_vma=False,
    )
```

time: 38.7 us -> 36.1 us (0.933)
  local copies, waits for them, and re-layouts: 2.24 us -> 0 us
  Pallas kernels: 35.7 us -> 33.8 us
  other arithmetic: 0 us -> 1.4 us
    pallas_call x1, Pallas kernels: 35.7 us -> 33.8 us  [per_device(): pl.pallas_call(kernel, name='dedup', out_shape=jax.ShapeDtypeStruct((9, 2...]
    unnamed x4 -> x0, local copies, waits for them, and re-layouts: 1.67 us -> none
    reduce_max x0 -> x1, other arithmetic: none -> 1.4 us  [per_device(): return (jnp.max(both[:, 0], axis=0), jnp.max(both[:, 1], axis=0))]
    slice x1 -> x0, local copies, waits for them, and re-layouts: 0.57 us -> none  [per_device(): return (both[0], both[1])]
where the time goes in v2:
time: 36.1 us; the launch traced here: 35.9 us
  Pallas kernels  33.8 us (94%)
  other arithmetic  1.4 us (4%)
  between operations  0.64 us (2%)
    pallas_call x1, Pallas kernels, per_device(): pl.pallas_call(kernel, name='dedup', out_shape=jax.ShapeDtypeStruct((9, 2...  33.8 us
    reduce_max x1, other arithmetic, per_device(): return (jnp.max(both[:, 0], axis=0), jnp.max(both[:, 1], axis=0))  1.4 us

profile of v2, /device:TPU:1, one launch (start us, length us, event | category | flops | bytes accessed | tf_op | source)
XLA Modules:
  0.0 35.9 jit_solution(18277510204284327041)
XLA Ops:
  0.6 33.8 %dedup.1 = f32[9,2,256]{2,1,0:T(2,128)} custom-call(bf16[256,768]{1,0:T(8,128)(2,1)} %emb.1, s32[1,256]{1,0:T(1,128)} %order.1), custom_call_target="tpu_custom_call" | custom-call | tf_op jit(solution)/shard_map/dedup/pallas_call | solution.py:275
  34.5 1.4 %slice_reduce_fusion = (f32[256]{0:T(256)}, f32[256]{0:T(256)}) fusion(f32[9,2,256]{2,1,0:T(2,128)} %dedup.1), kind=kLoop, calls=%fused_computation | loop fusion | flops 4096 | bytes 20480 | tf_op jit(solution)/shard_map/reduce_max | solution.py:291

commit v3 on v2

--- a/solution.py
+++ b/solution.py
@@ -7,9 +7,9 @@
 
 MESH = pl.DeviceIdType.MESH
 CHUNKS = 8
-LAG = CHUNKS // 2
+LAG = 5
 OPEN = 2
-DELTA = 3
+DELTA = 2
 YS = 8
 
 
@@ -166,7 +166,38 @@
         if 0 <= k - DELTA < CHUNKS:
             pl.when(late)(lambda: take(k - DELTA))
 
+    def pick(flag, v):
+        return jnp.where(flag, v, neg)
+
+    def top(*vs):
+        o = vs[0]
+        for v in vs[1:]:
+            o = jnp.maximum(o, v)
+        return o
+
+    def meet(a, blocks, col):
+        r = None
+        for j in range(2):
+            s = sims(a, blocks[j, ...])
+            col.append(colmax(s))
+            r = lanes(s) if r is None else jnp.maximum(r, lanes(s))
+        return r
+
+    at = lambda dy: (y + dy + YS) % YS
+    first0, first1, first2, first2e = at(0) < at(1), at(-1) < at(1), at(-2) < at(1), at(-2) < at(2)
+    col0, col1, col2, ecol = [], [], [], []
+
+    def near_products(prior0, later0):
+        c_own.wait_recv()
+        s01 = colmax(sims(own2[...], own[...]))
+        prior0 = top(prior0, pick(c == 1, s01))
+        later0 = top(later0, pick(c == 0, s01))
+        take_all(2, pc.at[0, 1 - c])
+        return prior0, later0, meet(own[...], pc.at[0], col0), meet(m1[...], pc.at[0], col1)
+
     for k in range(CHUNKS + LAG + DELTA):
+        if k == CHUNKS + LAG + DELTA - 1:
+            prior0, later0, r0, r1 = near_products(prior0, later0)
         if k == OPEN:
             pl.when(even)(lambda: pl.semaphore_wait(hello.at[2], 1))
             when(even, *c_c1[:OPEN])
@@ -174,92 +205,57 @@
         turn(late_p1, take_p1, k)
         turn(late_c1, take_c1, k - LAG)
 
-    c_own.wait_recv()
-    s01 = colmax(sims(own2[...], own[...]))
-    prior0 = jnp.maximum(prior0, jnp.where(c == 1, s01, neg))
-    later0 = jnp.maximum(later0, jnp.where(c == 0, s01, neg))
-
-    take_all(2, pc.at[0, 1 - c])
-
-    def meet(a, kind, col):
-        r = None
-        for j in range(2):
-            s = sims(a, pc[kind, j])
-            col.append(colmax(s))
-            r = lanes(s) if r is None else jnp.maximum(r, lanes(s))
-        return r
-
-    col0, col1, col2 = [], [], []
-    r0 = meet(own[...], 0, col0)
-    r1 = meet(m1[...], 0, col1)
     take_all(3, pc.at[1, 1 - c])
-    r0 = jnp.maximum(r0, meet(own[...], 1, col0))
-    r1 = jnp.maximum(r1, meet(m1[...], 1, col1))
+    r0 = flip(top(r0, meet(own[...], pc.at[1], col0)))
+    r1 = flip(top(r1, meet(m1[...], pc.at[1], col1)))
     other = (c + h) % 2
     pblk, cblk = pc[0, c], pc[1, other]
     pcol = colmax(sims(cblk, pblk))
     ccol = colmax(sims(pblk, cblk))
-    r0, r1 = flip(r0), flip(r1)
-
     for k in range(CHUNKS):
         c_e[k].wait_recv()
         n_e[k].start()
-    take_all(0, m2)
-    r2 = meet(m2[...], 0, col2)
-    r2 = flip(jnp.maximum(r2, meet(m2[...], 1, col2)))
-    ecol, re = [], None
-    take_all(4, e.at[1 - c])
-    for j in range(2):
-        s = sims(m2[...], e[j])
-        ecol.append(colmax(s))
-        re = lanes(s) if re is None else jnp.maximum(re, lanes(s))
-    re = flip(re)
-
-    at = lambda dy: (y + dy + YS) % YS
-    first0, first1, first2, first2e = at(0) < at(1), at(-1) < at(1), at(-2) < at(1), at(-2) < at(2)
-
-    def pick(flag, v):
-        return jnp.where(flag, v, neg)
-
-    def top(*vs):
-        o = vs[0]
-        for v in vs[1:]:
-            o = jnp.maximum(o, v)
-        return o
-
-    prior0 = top(prior0, pick(~first0, r0))
-    later0 = top(later0, pick(first0, r0))
 
     def put(i, prior, later):
         msg_out[i, 0:1, :] = jnp.maximum(prior, neg)
         msg_out[i, 1:2, :] = jnp.maximum(later, neg)
 
+    def post(i, slot, d):
+        copy(msg_out.at[i], out.at[slot], 9, r_all.at[5], d).start()
+
     put(0, pick(~first1, r1), pick(first1, r1))
-    put(1, top(pick(~first2, r2), pick(~first2e, re)), top(pick(first2, r2), pick(first2e, re)))
-    for j in range(2):
-        x = [col0[j], col1[j], col2[j]]
-        mine = pick(c == j, pcol)
-        put(2 + j,
-            top(pick(h == 1, mine), *[pick(f, v) for f, v in zip((first0, first1, first2), x)]),
-            top(pick(h == 0, mine), *[pick(~f, v) for f, v in zip((first0, first1, first2), x)]))
-        x = [col0[2 + j], col1[2 + j], col2[2 + j]]
-        mine = pick(other == j, ccol)
-        put(4 + j,
-            top(pick(h == 0, mine), *[pick(f, v) for f, v in zip((first0, first1, first2), x)]),
-            top(pick(h == 1, mine), *[pick(~f, v) for f, v in zip((first0, first1, first2), x)]))
-        put(6 + j, pick(first2e, ecol[j]), pick(~first2e, ecol[j]))
-
-    put(8, prior0, later0)
+    put(8, top(prior0, pick(~first0, r0)), top(later0, pick(first0, r0)))
+    post(0, 0, dev(-1, h, c))
     mine_out = pltpu.make_async_copy(msg_out.at[8], out.at[8], csem.at[0])
     mine_out.start()
+    before, after = [], []
+    for j in range(4):
+        mine = pick(c == j, pcol) if j < 2 else pick(other == j - 2, ccol)
+        home = h if j < 2 else 1 - h
+        before.append(top(pick(home == 1, mine), pick(first0, col0[j]), pick(first1, col1[j])))
+        after.append(top(pick(home == 0, mine), pick(~first0, col0[j]), pick(~first1, col1[j])))
+
+    take_all(0, m2)
+    r2 = meet(m2[...], pc.at[1], col2)
+    for j in range(2):
+        put(4 + j, top(before[2 + j], pick(first2, col2[j])), top(after[2 + j], pick(~first2, col2[j])))
+    post(4, 4 + c, dev(1, 1 - h, 0))
+    post(5, 4 + c, dev(1, 1 - h, 1))
+    r2 = top(r2, meet(m2[...], pc.at[0], col2))
+    take_all(4, e.at[1 - c])
+    re = meet(m2[...], e, ecol)
     he = (h + ((y + 2) % YS) // 4) % 2
-    for i, slot, d in [
-        (0, 0, dev(-1, h, c)), (1, 1, dev(-2, h, c)),
-        (2, 2 + c, dev(1, h, 0)), (3, 2 + c, dev(1, h, 1)),
-        (4, 4 + c, dev(1, 1 - h, 0)), (5, 4 + c, dev(1, 1 - h, 1)),
-        (6, 6 + c, dev(2, he, 0)), (7, 6 + c, dev(2, he, 1)),
-    ]:
-        copy(msg_out.at[i], out.at[slot], 9, r_all.at[5], d).start()
+    for j in range(2):
+        put(6 + j, pick(first2e, ecol[j]), pick(~first2e, ecol[j]))
+    post(6, 6 + c, dev(2, he, 0))
+    post(7, 6 + c, dev(2, he, 1))
+    r2, re = flip(r2), flip(re)
+    put(1, top(pick(~first2, r2), pick(~first2e, re)), top(pick(first2, r2), pick(first2e, re)))
+    post(1, 1, dev(-2, h, c))
+    for j in range(2):
+        put(2 + j, top(before[j], pick(first2, col2[2 + j])), top(after[j], pick(~first2, col2[2 + j])))
+    post(2, 2 + c, dev(1, h, 0))
+    post(3, 2 + c, dev(1, h, 1))
     copy(msg_out.at[0:8], out.at[0:8], 9, r_all.at[5], up).wait_recv()
     for stream in range(9):
         copy(own, m1, stream, r_all.at[0], up).wait_send()

time: 36.1 us -> 33.2 us (0.920)
  Pallas kernels: 33.8 us -> 30.9 us
    pallas_call x1, Pallas kernels: 33.8 us -> 30.9 us  [per_device(): pl.pallas_call(kernel, name='dedup', out_shape=jax.ShapeDtypeStruct((9, 2...]
where the time goes in v3:
time: 33.2 us; the launch traced here: 32.9 us
  Pallas kernels  30.9 us (93%)
  other arithmetic  1.4 us (4%)
  between operations  0.64 us (2%)
    pallas_call x1, Pallas kernels, per_device(): pl.pallas_call(kernel, name='dedup', out_shape=jax.ShapeDtypeStruct((9, 2...  30.9 us
    reduce_max x1, other arithmetic, per_device(): return (jnp.max(both[:, 0], axis=0), jnp.max(both[:, 1], axis=0))  1.4 us

profile of v3, /device:TPU:1, one launch (start us, length us, event | category | flops | bytes accessed | tf_op | source)
XLA Modules:
  0.0 32.9 jit_solution(6463034956605618132)
XLA Ops:
  0.6 30.9 %dedup.1 = f32[9,2,256]{2,1,0:T(2,128)} custom-call(bf16[256,768]{1,0:T(8,128)(2,1)} %emb.1, s32[1,256]{1,0:T(1,128)} %order.1), custom_call_target="tpu_custom_call" | custom-call | tf_op jit(solution)/shard_map/dedup/pallas_call | solution.py:271
  31.5 1.4 %slice_reduce_fusion = (f32[256]{0:T(256)}, f32[256]{0:T(256)}) fusion(f32[9,2,256]{2,1,0:T(2,128)} %dedup.1), kind=kLoop, calls=%fused_computation | loop fusion | flops 4096 | bytes 20480 | tf_op jit(solution)/shard_map/reduce_max | solution.py:287

commit v4 on v3

--- a/solution.py
+++ b/solution.py
@@ -114,12 +114,12 @@
         for one in c_p1:
             one.start()
 
-    @pl.when(odd & (y < YS // 2))
+    @pl.when(odd & (y <= YS // 2))
     def _():
         open_up()
         open_down()
 
-    @pl.when(odd & (y >= YS // 2))
+    @pl.when(odd & (y > YS // 2))
     def _():
         open_down()
         open_up()
@@ -281,9 +281,12 @@
             pltpu.SemaphoreType.REGULAR((4,)), dma(2), dma(10), dma(4, CHUNKS), dma(6),
         ],
         compiler_params=pltpu.CompilerParams(
-            collective_id=0, has_side_effects=True
+            collective_id=0, has_side_effects=True, vmem_limit_bytes=55000 * 1024
         ),
-    )(embeddings, doc_order)
+    )(
+        pltpu.with_memory_space_constraint(embeddings, pltpu.HBM),
+        pltpu.with_memory_space_constraint(doc_order, pltpu.HBM),
+    )
     return jnp.max(both[:, 0], axis=0), jnp.max(both[:, 1], axis=0)
 
 

time: 33.2 us -> 32.3 us (0.973)
  other arithmetic: 1.4 us -> 0.6 us
    reduce_max x1, other arithmetic: 1.4 us -> 0.6 us  [per_device(): return (jnp.max(both[:, 0], axis=0), jnp.max(both[:, 1], axis=0))]
where the time goes in v4:
time: 32.3 us; the launch traced here: 32 us
  Pallas kernels  30.8 us (95%)
  between operations  0.64 us (2%)
  other arithmetic  0.6 us (2%)
    pallas_call x1, Pallas kernels, per_device(): pl.pallas_call(kernel, name='dedup', out_shape=jax.ShapeDtypeStruct((9, 2...  30.8 us

profile of v4, /device:TPU:1, one launch (start us, length us, event | category | flops | bytes accessed | tf_op | source)
XLA Modules:
  0.0 32.0 jit_solution(5590877980939120132)
XLA Ops:
  0.6 30.8 %dedup.1 = f32[9,2,256]{2,1,0:T(2,128)S(1)} custom-call(bf16[256,768]{1,0:T(8,128)(2,1)} %emb.1, s32[1,256]{1,0:T(1,128)} %order.1), custom_call_target="tpu_custom_call" | custom-call | tf_op jit(solution)/shard_map/dedup/pallas_call | solution.py:271
  31.4 0.6 %slice_reduce_fusion = (f32[256]{0:T(256)}, f32[256]{0:T(256)}) fusion(f32[9,2,256]{2,1,0:T(2,128)S(1)} %dedup.1), kind=kLoop, calls=%fused_computation | loop fusion | flops 4096 | bytes 20480 | tf_op jit(solution)/shard_map/reduce_max | solution.py:290

commit v5 on v4

--- a/solution.py
+++ b/solution.py
@@ -8,8 +8,8 @@
 MESH = pl.DeviceIdType.MESH
 CHUNKS = 8
 LAG = 5
-OPEN = 2
-DELTA = 2
+OPEN = 1
+DELTA = 3
 YS = 8
 
 
@@ -54,6 +54,7 @@
     corner = (clus == 0) & (c == 0)
     late_m1 = corner & (h == 0) & (y == 1)
     late_p1 = corner & (h == 0) & (y == YS - 1)
+    slow = (clus == 0) & ((y == 0) | (y == YS - 1))
     late_c1 = corner & (h == 1) & ((y == 0) | (y == YS - 1))
 
     def signal(sem, *devices):
@@ -203,7 +204,12 @@
             when(even, *c_c1[:OPEN])
         turn(late_m1, take_m1, k)
         turn(late_p1, take_p1, k)
-        turn(late_c1, take_c1, k - LAG)
+        if 0 <= k - LAG + 1 < CHUNKS:
+            pl.when(no(slow))(lambda: take_c1(k - LAG + 1))
+        if 0 <= k - LAG < CHUNKS:
+            pl.when(slow & no(late_c1))(lambda: take_c1(k - LAG))
+        if 0 <= k - LAG - DELTA < CHUNKS:
+            pl.when(late_c1)(lambda: take_c1(k - LAG - DELTA))
 
     take_all(3, pc.at[1, 1 - c])
     r0 = flip(top(r0, meet(own[...], pc.at[1], col0)))

time: 32.3 us -> 32.2 us (level)
  no operation moved by 1% of the time
where the time goes in v5:
time: 32.2 us; the launch traced here: 32 us
  Pallas kernels  30.8 us (96%)
  between operations  0.64 us (2%)
  other arithmetic  0.6 us (2%)
    pallas_call x1, Pallas kernels, per_device(): pl.pallas_call(kernel, name='dedup', out_shape=jax.ShapeDtypeStruct((9, 2...  30.8 us

profile of v5, /device:TPU:1, one launch (start us, length us, event | category | flops | bytes accessed | tf_op | source)
XLA Modules:
  0.0 32.0 jit_solution(5967736429933039402)
XLA Ops:
  0.6 30.8 %dedup.1 = f32[9,2,256]{2,1,0:T(2,128)S(1)} custom-call(bf16[256,768]{1,0:T(8,128)(2,1)} %emb.1, s32[1,256]{1,0:T(1,128)} %order.1), custom_call_target="tpu_custom_call" | custom-call | tf_op jit(solution)/shard_map/dedup/pallas_call | solution.py:277
  31.4 0.6 %slice_reduce_fusion = (f32[256]{0:T(256)}, f32[256]{0:T(256)}) fusion(f32[9,2,256]{2,1,0:T(2,128)S(1)} %dedup.1), kind=kLoop, calls=%fused_computation | loop fusion | flops 4096 | bytes 20480 | tf_op jit(solution)/shard_map/reduce_max | solution.py:296
